TPU v7x, 32 devices: a whole 2x2x4 slice. The times are simulated.
32 devices in a mesh: row: 8 (over y, x, core), col: 4 (over z).
Axes of the slice: x: 2, y: 2, z: 4, core: 2. Of those that a mesh axis runs over, the one named last changes fastest.
Arguments:
- source: float32 [512, 512, 512], P('row', 'col'), may hold values from -8 to 8
- basis_x: float32 [512, 512], replicated, may hold values from -0.25 to 0.25
- basis_y: float32 [512, 512], replicated, may hold values from -0.25 to 0.25
- basis_z: float32 [512, 512], replicated, may hold values from -0.25 to 0.25
- eigen_x: float32 [512], replicated, may hold values from 0.1 to 10
- eigen_y: float32 [512], replicated, may hold values from 0.1 to 10
- eigen_z: float32 [512], replicated, may hold values from 0.1 to 10
Outputs:
- solution: float32 [512, 512, 512], P('row', 'col')
All inputs are finite; a program needn't handle non-finite values.
Results may differ from a plain program's by a relative error of at most 0.00007.
Values sent between devices are 32-bit elements; how exact they have to be, the bound alone decides.
A program may use at most 128 MiB of HBM per device.

v0:
```python
import jax
import jax.numpy as jnp
from jax import lax
from jax.sharding import PartitionSpec as P

HIGH = lax.Precision.HIGHEST


def divide(field, first, second, third):
    denom = first[:, None, None] + second[None, :, None] + third[None, None, :]
    return field / denom


def piece_of(values, index, count):
    return lax.dynamic_slice_in_dim(values, index * count, count, 0)


def local(source, basis_x, basis_y, basis_z, eigen_x, eigen_y, eigen_z):
    row_index = lax.axis_index("row")
    col_index = lax.axis_index("col")
    rows_n = lax.axis_size("row")
    cols_n = lax.axis_size("col")
    nx_full = basis_x.shape[0]
    ny_full = basis_y.shape[0]
    field = jnp.einsum("ck,abc->abk", basis_z, source, precision=HIGH)
    field = field[None]
    field = lax.all_to_all(field, ("row", "col"), split_axis=3, concat_axis=0, tiled=True)
    planes = field.shape[3]
    field = field.reshape(rows_n, cols_n, field.shape[1], field.shape[2], planes)
    blocks_x = basis_x.reshape(rows_n, nx_full // rows_n, nx_full)
    blocks_y = basis_y.reshape(cols_n, ny_full // cols_n, ny_full)
    field = jnp.einsum("rai,rcabk->icbk", blocks_x, field, precision=HIGH)
    field = jnp.einsum("cbj,icbk->ijk", blocks_y, field, precision=HIGH)
    part_z = piece_of(eigen_z, row_index * cols_n + col_index, planes)
    field = divide(field, eigen_x, eigen_y, part_z)
    field = jnp.einsum("cbj,ijk->icbk", blocks_y, field, precision=HIGH)
    field = jnp.einsum("rai,icbk->rcabk", blocks_x, field, precision=HIGH)
    field = field.reshape(rows_n * cols_n, field.shape[2], field.shape[3], planes)
    field = lax.all_to_all(field, ("row", "col"), split_axis=0, concat_axis=3, tiled=True)
    field = jnp.einsum("ck,abk->abc", basis_z, field[0], precision=HIGH)
    return field


def solution(mesh):
    placed = (P("row", "col", None), P(), P(), P(), P(), P(), P())
    return jax.shard_map(
        local, mesh=mesh, in_specs=placed, out_specs=P("row", "col", None), check_vma=False
    )
```

profile of v0, /device:TPU:9, one launch (start us, length us, event | category | flops | bytes accessed | tf_op | source)
XLA Modules:
  0.0 1080.2 jit_solution(10844230199941101817)
XLA Ops:
  0.0 0.0 copy-start
  0.0 32.2 %convolution_bitcast_fusion.1 = f32[1,64,128,512]{3,2,1,0:T(8,128)} fusion(f32[64,128,512]{2,1,0:T(8,128)} %param.7, f32[512,512]{1,0:T(8,128)} %param.10), kind=kOutput, calls=%fused_computation.8 | convolution fusion | flops 25769803776 | bytes 34603008 | tf_op jit(solution)/shard_map/ck,abc->abk/dot_general | solution.py:25
  32.2 16.5 %copy.19 = f32[1,64,128,512]{2,1,0,3:T(8,128)} copy(f32[1,64,128,512]{3,2,1,0:T(8,128)} %convolution_bitcast_fusion.1) | data formatting | bytes 33554432 | tf_op jit(solution)/shard_map/broadcast_in_dim | solution.py:26
  48.7 0.0 copy-start.3
  48.7 0.0 copy-start.4
  48.7 6.7 all-to-all-start
  55.5 0.8 dynamic_slice.3
  56.2 0.0 copy-done.3
  56.2 0.0 copy-done.4
  56.2 0.1 broadcast_add_fusion
  56.4 369.3 %all-to-all-done = f32[1,64,128,512]{2,1,0,3:T(8,128)} async-done(((f32[1,64,128,512]{2,1,0,3:T(8,128)}), f32[1,64,128,512]{2,1,0,3:T(8,128)}, u32[]{:S(2)}, u32[]{:S(2)}) %all-to-all-start) | async-done | bytes 16777248 | tf_op jit(solution)/shard_map/all_to_all | solution.py:27
  425.7 0.0 copy-start.2
  425.7 30.6 %copy.22 = f32[8,4,64,128,16]{2,4,0,3,1:T(8,128)} copy(f32[8,4,64,128,16]{3,2,4,1,0:T(8,128)} %bitcast.29) | data formatting | bytes 33554432 | tf_op jit(solution)/shard_map/reshape | solution.py:29
  456.2 0.0 copy-done.2
  456.2 50.3 %convolution_bitcast_fusion = f32[512,4,128,16]{0,3,2,1:T(8,128)} fusion(f32[8,4,64,128,16]{2,4,0,3,1:T(8,128)} %copy.22, f32[8,64,512,1,1]{2,1,0,4,3:T(8,128)S(1)} %bitcast.65), kind=kOutput, calls=%fused_computation.7 | convolution fusion | flops 25769803776 | bytes 34603008 | tf_op jit(solution)/shard_map/rai,rcabk->icbk/dot_general | solution.py:32
  506.5 20.7 %copy.23 = f32[512,4,128,16]{2,3,1,0:T(8,128)} copy(f32[512,4,128,16]{0,3,2,1:T(8,128)} %convolution_bitcast_fusion) | data formatting | bytes 33554432 | tf_op jit(solution)/shard_map/rai,rcabk->icbk/dot_general | solution.py:32
  527.2 0.0 copy-done
  527.2 31.9 %bitcast_divide_fusion = f32[512,512,16]{1,2,0:T(8,128)} fusion(f32[512,4,128,16]{2,3,1,0:T(8,128)} %copy.23, f32[4,128,512,1]{2,1,0,3:T(8,128)S(1)} %bitcast.61, f32[16]{0:T(128)S(1)} %dynamic_slice.3, f32[512,512]{1,0:T(8,128)S(1)} %broadcast_add_fusion), kind=kOutput, calls=%fused_computation.2 | convolution fusion | flops 25778192384 | bytes 35651648 | tf_op jit(solution)/shard_map/cbj,icbk->ijk/dot_general | solution.py:33
  559.1 41.4 %fusion.2 = f32[512,16,4,128]{3,0,1,2:T(8,128)S(1)} fusion(f32[4,128,512,1]{2,1,3,0:T(8,128)S(1)} %bitcast.60, f32[512,512,16]{1,2,0:T(8,128)} %bitcast_divide_fusion), kind=kOutput, calls=%fused_computation.3 | convolution fusion | flops 25769803776 | bytes 34603008 | tf_op jit(solution)/shard_map/cbj,ijk->icbk/dot_general | solution.py:36
  600.6 30.2 %fusion.5 = f32[8,4,64,128,16]{3,2,0,4,1:T(8,128)} fusion(f32[8,64,512,1,1]{2,1,0,4,3:T(8,128)S(1)} %bitcast.66, f32[512,16,4,128]{3,0,1,2:T(8,128)S(1)} %fusion.2), kind=kOutput, calls=%fused_computation.6 | convolution fusion | flops 25769803776 | bytes 34603008 | tf_op jit(solution)/shard_map/rai,icbk->rcabk/dot_general | solution.py:37
  630.8 16.9 %copy.25 = f32[8,4,64,128,16]{3,4,2,1,0:T(8,128)S(1)} copy(f32[8,4,64,128,16]{3,2,0,4,1:T(8,128)} %fusion.5) | data formatting | bytes 33554432 | tf_op jit(solution)/shard_map/rai,icbk->rcabk/transpose | solution.py:37
  647.6 366.7 %all_to_all.30 = f32[32,64,128,16]{2,3,1,0:T(8,128)} all-to-all(f32[32,64,128,16]{2,3,1,0:T(8,128)S(1)} %bitcast.63), channel_id=1, replica_groups=mesh['row'=8,'col'=4] {'row','col'}, dimensions={0} | all-to-all | bytes 33554432 | tf_op jit(solution)/shard_map/all_to_all | solution.py:39
  1014.4 0.0 copy-start.1
  1014.4 6.9 copy.26
  1021.3 0.0 copy-done.1
  1021.3 58.6 %fusion.8 = f32[64,128,512]{2,1,0:T(8,128)} fusion(f32[64,128,512]{1,2,0:T(8,128)S(1)} %bitcast.62, f32[512,512]{1,0:T(8,128)S(1)} %copy-done.1), kind=kOutput, calls=%fused_computation.9 | convolution fusion | flops 25769803776 | bytes 34603008 | tf_op jit(solution)/shard_map/ck,abk->abc/dot_general | solution.py:40
Async XLA Ops:
  0.0 527.2 %copy-start = (f32[512,512]{1,0:T(8,128)S(1)}, f32[512,512]{1,0:T(8,128)}, u32[]{:S(2)}) copy-start(f32[512,512]{1,0:T(8,128)} %param.9) | copy-start | bytes 3145732
  48.7 7.5 copy-start.3
  48.7 7.5 copy-start.4
  48.7 377.0 %all-to-all-start = ((f32[1,64,128,512]{2,1,0,3:T(8,128)}), f32[1,64,128,512]{2,1,0,3:T(8,128)}, u32[]{:S(2)}, u32[]{:S(2)}) async-start(f32[1,64,128,512]{2,1,0,3:T(8,128)} %copy.19), calls=%async_computation | async-start | bytes 33554432 | tf_op jit(solution)/shard_map/all_to_all | solution.py:27
  425.7 30.6 %copy-start.2 = (f32[512,512]{1,0:T(8,128)S(1)}, f32[512,512]{1,0:T(8,128)}, u32[]{:S(2)}) copy-start(f32[512,512]{1,0:T(8,128)} %param.8) | copy-start | bytes 3145732
  1014.4 6.9 copy-start.1
where the time goes:
time: 1090 us; the launch traced here: 1080 us
  waiting for transfers between devices  369 us (34%)
  blocking collectives  367 us (34%)
  matrix products  245 us (22%)
  local copies, waits for them, and re-layouts  92.4 us (8%)
    all_to_all x1, waiting for transfers between devices, local(): lax.all_to_all(field, ('row', 'col'), split_axis=3, concat_axis=0, tiled=...  369 us
    all_to_all x1, blocking collectives, local(): lax.all_to_all(field, ('row', 'col'), split_axis=0, concat_axis=3, tiled=...  367 us
    dot_general x1, matrix products, local(): field = jnp.einsum('ck,abk->abc', basis_z, field[0], precision=HIGH)  58.6 us
    dot_general x1, matrix products, local(): field = jnp.einsum('rai,rcabk->icbk', blocks_x, field, precision=HIGH)  50.3 us
    dot_general x1, matrix products, local(): field = jnp.einsum('cbj,ijk->icbk', blocks_y, field, precision=HIGH)  41.4 us
    dot_general x1, matrix products, local(): field = jnp.einsum('ck,abc->abk', basis_z, source, precision=HIGH)  32.2 us
    dot_general x1, matrix products, local(): field = jnp.einsum('cbj,icbk->ijk', blocks_y, field, precision=HIGH)  31.9 us
    reshape x1, local copies, waits for them, and re-layouts, local(): field.reshape(rows_n, cols_n, field.shape[1], field.shape[2], planes)  30.6 us
  transfers between devices with their start and end apart: 1, of which 1 were waited for; matrix products, arithmetic and copies ran while one was open for 0% of the time, Pallas kernels for 0%

commit v1 on v0

v1 whole, which is shorter than its diff:
```python
import math

import jax
import jax.numpy as jnp
from jax import lax
from jax.sharding import PartitionSpec as P

PREC = lax.Precision.HIGH
CHUNKS = 4


def local(source, basis_x, basis_y, basis_z, eigen_x, eigen_y, eigen_z):
    rows_n = lax.axis_size("row")
    cols_n = lax.axis_size("col")
    devices = rows_n * cols_n
    me = lax.axis_index("row") * cols_n + lax.axis_index("col")
    ax, by, nz = source.shape
    nx, ny = basis_x.shape[0], basis_y.shape[0]
    planes = nz // devices
    chunks = math.gcd(CHUNKS, planes)
    step = planes // chunks
    bz = basis_z.reshape(nz, devices, chunks, step)
    ez = lax.dynamic_slice_in_dim(eigen_z, me * planes, planes, 0).reshape(chunks, step)
    exy = eigen_x[:, None] + eigen_y[None, :]

    def forward(c):
        part = bz[:, :, c, :].reshape(nz, devices * step)
        field = jnp.einsum("ck,abc->kab", part, source, precision=PREC)
        return lax.all_to_all(field, ("row", "col"), split_axis=0, concat_axis=0, tiled=True)

    def middle(c, field):
        field = field.reshape(rows_n, cols_n, step, ax, by)
        field = field.transpose(2, 0, 3, 1, 4).reshape(step, nx, ny)
        field = jnp.einsum("xi,kxy->kiy", basis_x, field, precision=PREC)
        field = jnp.einsum("kiy,yj->kij", field, basis_y, precision=PREC)
        field = field / (exy[None] + ez[c][:, None, None])
        field = jnp.einsum("kij,yj->kiy", field, basis_y, precision=PREC)
        field = jnp.einsum("xi,kiy->kxy", basis_x, field, precision=PREC)
        field = field.reshape(step, rows_n, ax, cols_n, by).transpose(1, 3, 0, 2, 4)
        field = field.reshape(devices * step, ax, by)
        return lax.all_to_all(field, ("row", "col"), split_axis=0, concat_axis=0, tiled=True)

    def backward(c, field):
        part = bz[:, :, c, :].reshape(nz, devices * step)
        return jnp.einsum("ck,kab->abc", part, field, precision=PREC)

    arrived = [forward(c) for c in range(chunks)]
    returned = [middle(c, arrived[c]) for c in range(chunks)]
    out = backward(0, returned[0])
    for c in range(1, chunks):
        out = out + backward(c, returned[c])
    return out


def solution(mesh):
    placed = (P("row", "col", None), P(), P(), P(), P(), P(), P())
    return jax.shard_map(
        local, mesh=mesh, in_specs=placed, out_specs=P("row", "col", None), check_vma=False
    )
```

time: 1090 us -> 846 us (0.78)
  blocking collectives: 367 us -> 0 us
  waiting for transfers between devices: 369 us -> 459 us
  local copies, waits for them, and re-layouts: 92.4 us -> 135 us
  matrix products: 245 us -> 207 us
  starting transfers between devices: 6.74 us -> 36.5 us
    all_to_all x1 -> x0, blocking collectives: 367 us -> none  [local(): lax.all_to_all(field, ('row', 'col'), split_axis=0, concat_axis=3, tiled=...]
    all_to_all x1 -> x8, waiting for transfers between devices: 369 us -> 459 us  [the longest x4 278 us: forward(): lax.all_to_all(field, ('row', 'col'), split_axis=0, concat_axis=0, tiled=...]
    reshape x1 -> x13, local copies, waits for them, and re-layouts: 30.6 us -> 74.3 us  [the longest x4 31.2 us: middle(): field = field.reshape(rows_n, cols_n, step, ax, by)]
    dot_general x6 -> x24, matrix products: 245 us -> 207 us  [the longest x4 87.5 us: backward(): return jnp.einsum('ck,kab->abc', part, field, precision=PREC)]
    all_to_all x1 -> x8, starting transfers between devices: 6.74 us -> 36.5 us  [the longest x4 19.5 us: forward(): lax.all_to_all(field, ('row', 'col'), split_axis=0, concat_axis=0, tiled=...]
    transpose x1 -> x8, local copies, waits for them, and re-layouts: 16.9 us -> 40.1 us  [the longest x4 21 us: middle(): field = jnp.einsum('xi,kiy->kxy', basis_x, field, precision=PREC)]
    broadcast_in_dim x1 -> x0, local copies, waits for them, and re-layouts: 16.5 us -> none  [local(): field = field[None]]
  transfers between devices with their start and end apart: 1 -> 8, of which waited for: 1 -> 8; matrix products, arithmetic and copies ran while one was open for 0% -> 35% of each run, Pallas kernels for 0% -> 0%
where the time goes in v1:
time: 846 us; the launch traced here: 839 us
  waiting for transfers between devices  459 us (54%)
  matrix products  207 us (24%)
  local copies, waits for them, and re-layouts  135 us (16%)
  starting transfers between devices  36.5 us (4%)
    all_to_all x4, waiting for transfers between devices, forward(): lax.all_to_all(field, ('row', 'col'), split_axis=0, concat_axis=0, tiled=...  278 us
    all_to_all x4, waiting for transfers between devices, middle(): lax.all_to_all(field, ('row', 'col'), split_axis=0, concat_axis=0, tiled=...  181 us
    dot_general x4, matrix products, backward(): return jnp.einsum('ck,kab->abc', part, field, precision=PREC)  87.5 us
    dot_general x4, matrix products, forward(): field = jnp.einsum('ck,abc->kab', part, source, precision=PREC)  47.7 us
    reshape x4, local copies, waits for them, and re-layouts, middle(): field = field.reshape(rows_n, cols_n, step, ax, by)  31.2 us
    dot_general x4, matrix products, middle(): field = jnp.einsum('xi,kxy->kiy', basis_x, field, precision=PREC)  22 us
    reshape x4, local copies, waits for them, and re-layouts, middle(): field = field.transpose(2, 0, 3, 1, 4).reshape(step, nx, ny)  21.9 us
    transpose x4, local copies, waits for them, and re-layouts, middle(): field = jnp.einsum('xi,kiy->kxy', basis_x, field, precision=PREC)  21 us
  transfers between devices with their start and end apart: 8, of which 8 were waited for; matrix products, arithmetic and copies ran while one was open for 35% of the time, Pallas kernels for 0%

profile of v1, /device:TPU:9, one launch (start us, length us, event | category | flops | bytes accessed | tf_op | source)
XLA Modules:
  0.0 839.2 jit_solution(302734096856918325)
XLA Ops:
  2.2 11.9 %fusion.61 = f32[128,64,128]{2,0,1:T(8,128)S(1)} fusion(f32[512,128,1]{0,1,2:T(8,128)S(1)} %reshape.108, f32[64,128,512]{2,1,0:T(8,128)} %param.7), kind=kOutput, calls=%fused_computation.71 | convolution fusion | flops 3221225472 | bytes 21233664 | tf_op jit(solution)/shard_map/ck,abc->kab/dot_general | solution.py:28
  14.1 4.4 copy.42
  18.6 6.9 all-to-all-start
  25.5 11.9 %fusion.62 = f32[128,64,128]{2,0,1:T(8,128)S(1)} fusion(f32[512,128,1]{0,1,2:T(8,128)S(1)} %reshape.112, f32[64,128,512]{2,1,0:T(8,128)} %param.7), kind=kOutput, calls=%fused_computation.72 | convolution fusion | flops 3221225472 | bytes 21233664 | tf_op jit(solution)/shard_map/ck,abc->kab/dot_general | solution.py:28
  41.8 77.5 %all-to-all-done = f32[128,64,128]{2,1,0:T(8,128)} async-done(((f32[128,64,128]{2,1,0:T(8,128)}), f32[128,64,128]{2,1,0:T(8,128)}, u32[]{:S(2)}, u32[]{:S(2)}) %all-to-all-start) | async-done | bytes 4194336 | tf_op jit(solution)/shard_map/all_to_all | solution.py:29
  119.4 4.4 all-to-all-start.2
  123.9 11.9 %fusion.63 = f32[128,64,128]{2,0,1:T(8,128)S(1)} fusion(f32[512,128,1]{0,1,2:T(8,128)S(1)} %reshape.114, f32[64,128,512]{2,1,0:T(8,128)} %param.7), kind=kOutput, calls=%fused_computation.73 | convolution fusion | flops 3221225472 | bytes 21233664 | tf_op jit(solution)/shard_map/ck,abc->kab/dot_general | solution.py:28
  135.9 4.4 copy.60
  140.3 77.5 %all-to-all-done.2 = f32[128,64,128]{2,1,0:T(8,128)} async-done(((f32[128,64,128]{2,1,0:T(8,128)}), f32[128,64,128]{2,1,0:T(8,128)}, u32[]{:S(2)}, u32[]{:S(2)}) %all-to-all-start.2) | async-done | bytes 4194336 | tf_op jit(solution)/shard_map/all_to_all | solution.py:29
  222.0 11.9 %fusion.64 = f32[128,64,128]{2,0,1:T(8,128)S(1)} fusion(f32[512,128,1]{0,1,2:T(8,128)S(1)} %reshape.116, f32[64,128,512]{2,1,0:T(8,128)} %param.7), kind=kOutput, calls=%fused_computation.74 | convolution fusion | flops 3221225472 | bytes 21233664 | tf_op jit(solution)/shard_map/ck,abc->kab/dot_general | solution.py:28
  238.3 77.5 %all-to-all-done.4 = f32[128,64,128]{2,1,0:T(8,128)} async-done(((f32[128,64,128]{2,1,0:T(8,128)}), f32[128,64,128]{2,1,0:T(8,128)}, u32[]{:S(2)}, u32[]{:S(2)}) %all-to-all-start.4) | async-done | bytes 4194336 | tf_op jit(solution)/shard_map/all_to_all | solution.py:29
  322.0 7.8 copy.113
  329.8 5.5 reshape.93
  335.3 5.5 fusion.53
  348.3 5.0 convolution_bitcast_fusion.3
  353.3 5.2 copy.47
  358.5 5.2 reshape.94
  363.7 4.7 copy.48
  368.5 45.5 %all-to-all-done.6 = f32[128,64,128]{2,1,0:T(8,128)} async-done(((f32[128,64,128]{2,1,0:T(8,128)}), f32[128,64,128]{2,1,0:T(8,128)}, u32[]{:S(2)}, u32[]{:S(2)}) %all-to-all-start.6) | async-done | bytes 4194336 | tf_op jit(solution)/shard_map/all_to_all | solution.py:29
  418.3 7.8 copy.112
  426.1 5.5 reshape.97
  431.6 5.5 fusion.50
  444.4 5.0 convolution_bitcast_fusion.2
  449.4 5.3 copy.56
  454.7 5.2 reshape.98
  459.9 4.8 copy.57
  464.7 47.5 %all-to-all-done.1 = f32[128,64,128]{2,1,0:T(8,128)} async-done(((f32[128,64,128]{2,1,0:T(8,128)}), f32[128,64,128]{2,1,0:T(8,128)}, u32[]{:S(2)}, u32[]{:S(2)}) %all-to-all-start.1) | async-done | bytes 4194336 | tf_op jit(solution)/shard_map/all_to_all | solution.py:41
  516.4 7.8 copy.111
  524.2 5.5 reshape.101
  529.7 5.6 fusion.47
  542.6 5.0 convolution_bitcast_fusion.1
  547.6 5.3 copy.65
  552.9 5.2 reshape.102
  558.1 4.8 copy.66
  562.9 47.5 %all-to-all-done.3 = f32[128,64,128]{2,1,0:T(8,128)} async-done(((f32[128,64,128]{2,1,0:T(8,128)}), f32[128,64,128]{2,1,0:T(8,128)}, u32[]{:S(2)}, u32[]{:S(2)}) %all-to-all-start.3) | async-done | bytes 4194336 | tf_op jit(solution)/shard_map/all_to_all | solution.py:41
  614.8 7.8 copy.110
  622.6 5.4 reshape.105
  628.0 5.5 fusion.44
  640.8 5.0 convolution_bitcast_fusion
  645.9 5.2 copy.74
  651.1 5.2 reshape.106
  656.3 4.8 copy.75
  661.1 47.6 %all-to-all-done.5 = f32[128,64,128]{2,1,0:T(8,128)} async-done(((f32[128,64,128]{2,1,0:T(8,128)}), f32[128,64,128]{2,1,0:T(8,128)}, u32[]{:S(2)}, u32[]{:S(2)}) %all-to-all-start.5) | async-done | bytes 4194336 | tf_op jit(solution)/shard_map/all_to_all | solution.py:41
  713.3 18.5 %fusion.9 = f32[64,128,512]{2,1,0:T(8,128)} fusion(f32[128,64,128]{2,1,0:T(8,128)} %all-to-all-done.5, f32[512,128]{0,1:T(8,128)S(1)} %reshape_squeeze.18), kind=kOutput, calls=%fused_computation.11 | convolution fusion | flops 3221225472 | bytes 21233664 | tf_op jit(solution)/shard_map/ck,kab->abc/dot_general | solution.py:45
  731.7 18.4 %fusion.11 = f32[64,128,512]{2,1,0:T(8,128)} fusion(f32[128,64,128]{2,1,0:T(8,128)} %all-to-all-done.3, f32[512,128]{0,1:T(8,128)S(1)} %reshape_squeeze.17), kind=kOutput, calls=%fused_computation.14 | convolution fusion | flops 3221225472 | bytes 21233664 | tf_op jit(solution)/shard_map/ck,kab->abc/dot_general | solution.py:45
  750.1 18.7 %fusion.13 = f32[64,128,512]{2,1,0:T(8,128)} fusion(f32[128,64,128]{2,1,0:T(8,128)} %all-to-all-done.1, f32[512,128]{0,1:T(8,128)S(1)} %reshape_squeeze.16), kind=kOutput, calls=%fused_computation.17 | convolution fusion | flops 3221225472 | bytes 21233664 | tf_op jit(solution)/shard_map/ck,kab->abc/dot_general | solution.py:45
  768.8 38.0 %all-to-all-done.7 = f32[128,64,128]{2,1,0:T(8,128)} async-done(((f32[128,64,128]{2,1,0:T(8,128)}), f32[128,64,128]{2,1,0:T(8,128)}, u32[]{:S(2)}, u32[]{:S(2)}) %all-to-all-start.7) | async-done | bytes 4194336 | tf_op jit(solution)/shard_map/all_to_all | solution.py:41
  806.8 32.0 %add_add_fusion = f32[64,128,512]{2,1,0:T(8,128)} fusion(f32[64,128,512]{2,1,0:T(8,128)} %fusion.9, f32[64,128,512]{2,1,0:T(8,128)} %fusion.13, f32[64,128,512]{2,1,0:T(8,128)} %fusion.11, f32[128,64,128]{2,1,0:T(8,128)} %all-to-all-done.7, f32[512,128]{0,1:T(8,128)S(1)} %reshape_squeeze.19), kind=kOutput, calls=%fused_computation | convolution fusion | flops 3233808384 | bytes 71565312 | tf_op jit(solution)/shard_map/ck,kab->abc/dot_general | solution.py:45
  (50 shorter events, 68.0 us)
Async XLA Ops:
  0.0 340.9 %copy-start = (f32[512,512]{1,0:T(8,128)S(1)}, f32[512,512]{1,0:T(8,128)}, u32[]{:S(2)}) copy-start(f32[512,512]{1,0:T(8,128)} %param.9) | copy-start | bytes 3145732
  2.1 12.0 %copy-start.2 = (f32[512,32,1,4]{0,3,2,1:T(4,128)}, f32[512,32,1,4]{0,3,2,1:T(4,128)S(1)}, u32[]{:S(2)}) copy-start(f32[512,32,1,4]{0,3,2,1:T(4,128)S(1)} %get-tuple-element.8) | copy-start | bytes 786436
  18.6 100.8 %all-to-all-start = ((f32[128,64,128]{2,1,0:T(8,128)}), f32[128,64,128]{2,1,0:T(8,128)}, u32[]{:S(2)}, u32[]{:S(2)}) async-start(f32[128,64,128]{2,1,0:T(8,128)} %copy.42), calls=%async_computation | async-start | bytes 8388608 | tf_op jit(solution)/shard_map/all_to_all | solution.py:29
  119.4 98.4 %all-to-all-start.2 = ((f32[128,64,128]{2,1,0:T(8,128)}), f32[128,64,128]{2,1,0:T(8,128)}, u32[]{:S(2)}, u32[]{:S(2)}) async-start(f32[128,64,128]{2,1,0:T(8,128)} %copy.51), calls=%async_computation.2 | async-start | bytes 8388608 | tf_op jit(solution)/shard_map/all_to_all | solution.py:29
  217.8 98.1 %all-to-all-start.4 = ((f32[128,64,128]{2,1,0:T(8,128)}), f32[128,64,128]{2,1,0:T(8,128)}, u32[]{:S(2)}, u32[]{:S(2)}) async-start(f32[128,64,128]{2,1,0:T(8,128)} %copy.60), calls=%async_computation.4 | async-start | bytes 8388608 | tf_op jit(solution)/shard_map/all_to_all | solution.py:29
  238.3 82.5 %copy-start.8 = (f32[512]{0:T(512)S(1)}, f32[512]{0:T(512)}, u32[]{:S(2)}) copy-start(f32[512]{0:T(512)} %param.12) | copy-start | bytes 6148
  238.3 82.5 %copy-start.9 = (f32[512]{0:T(512)S(1)}, f32[512]{0:T(512)}, u32[]{:S(2)}) copy-start(f32[512]{0:T(512)} %param.11) | copy-start | bytes 6148
  315.8 98.1 %all-to-all-start.6 = ((f32[128,64,128]{2,1,0:T(8,128)}), f32[128,64,128]{2,1,0:T(8,128)}, u32[]{:S(2)}, u32[]{:S(2)}) async-start(f32[128,64,128]{2,1,0:T(8,128)} %copy.69), calls=%async_computation.6 | async-start | bytes 8388608 | tf_op jit(solution)/shard_map/all_to_all | solution.py:29
  329.8 5.6 copy-start.1
  340.9 3.5 copy-start.4
  413.9 98.3 %all-to-all-start.1 = ((f32[128,64,128]{2,1,0:T(8,128)}), f32[128,64,128]{2,1,0:T(8,128)}, u32[]{:S(2)}, u32[]{:S(2)}) async-start(f32[128,64,128]{2,1,0:T(8,128)} %bitcast.125), calls=%async_computation.1 | async-start | bytes 8388608 | tf_op jit(solution)/shard_map/all_to_all | solution.py:41
  437.1 3.5 copy-start.5
  512.3 98.1 %all-to-all-start.3 = ((f32[128,64,128]{2,1,0:T(8,128)}), f32[128,64,128]{2,1,0:T(8,128)}, u32[]{:S(2)}, u32[]{:S(2)}) async-start(f32[128,64,128]{2,1,0:T(8,128)} %bitcast.126), calls=%async_computation.3 | async-start | bytes 8388608 | tf_op jit(solution)/shard_map/all_to_all | solution.py:41
  535.2 3.5 copy-start.6
  610.4 98.3 %all-to-all-start.5 = ((f32[128,64,128]{2,1,0:T(8,128)}), f32[128,64,128]{2,1,0:T(8,128)}, u32[]{:S(2)}, u32[]{:S(2)}) async-start(f32[128,64,128]{2,1,0:T(8,128)} %bitcast.124), calls=%async_computation.5 | async-start | bytes 8388608 | tf_op jit(solution)/shard_map/all_to_all | solution.py:41
  633.5 3.5 copy-start.7
  708.7 4.4 copy-start.3
  708.7 98.1 %all-to-all-start.7 = ((f32[128,64,128]{2,1,0:T(8,128)}), f32[128,64,128]{2,1,0:T(8,128)}, u32[]{:S(2)}, u32[]{:S(2)}) async-start(f32[128,64,128]{2,1,0:T(8,128)} %bitcast.127), calls=%async_computation.7 | async-start | bytes 8388608 | tf_op jit(solution)/shard_map/all_to_all | solution.py:41

commit v2 on v1

v2 whole, which is shorter than its diff:
```python
import jax
import jax.numpy as jnp
from jax import lax
from jax.experimental.layout import Layout, with_layout_constraint
from jax.sharding import PartitionSpec as P

FAST = lax.Precision.HIGH
FULL = lax.Precision.HIGHEST


def cuts(planes):
    if planes < 3:
        return [(p, 1) for p in range(planes)]
    first = max(1, planes * 2 // 16)
    last = max(1, planes * 6 // 16)
    return [(0, first), (first, planes - first - last), (planes - last, last)]


def local(source, basis_x, basis_y, basis_z, eigen_x, eigen_y, eigen_z):
    rows_n = lax.axis_size("row")
    cols_n = lax.axis_size("col")
    devices = rows_n * cols_n
    me = lax.axis_index("row") * cols_n + lax.axis_index("col")
    ax, by, nz = source.shape
    nx, ny = basis_x.shape[0], basis_y.shape[0]
    planes = nz // devices
    bz = basis_z.reshape(nz, devices, planes)
    ez = lax.dynamic_slice_in_dim(eigen_z, me * planes, planes, 0)
    exy = eigen_x[:, None] + eigen_y[None, :]
    pieces = cuts(planes)

    def columns(piece):
        start, count = piece
        return bz[:, :, start : start + count].reshape(nz, devices * count)

    def exchange(field):
        return lax.all_to_all(field, ("row", "col"), split_axis=0, concat_axis=0, tiled=True)

    def forward(piece):
        field = jnp.einsum("ck,abc->kab", columns(piece), source, precision=FAST)
        return with_layout_constraint(field, Layout(major_to_minor=(0, 1, 2)))

    def middle(piece, field):
        start, count = piece
        field = field.reshape(rows_n, cols_n, count, ax, by)
        field = field.transpose(2, 0, 3, 1, 4).reshape(count, nx, ny)
        field = jnp.einsum("xi,kxy->kiy", basis_x, field, precision=FULL)
        field = jnp.einsum("kiy,yj->kij", field, basis_y, precision=FULL)
        field = field / (exy[None] + ez[start : start + count][:, None, None])
        field = jnp.einsum("kij,yj->kiy", field, basis_y, precision=FULL)
        field = jnp.einsum("xi,kiy->kxy", basis_x, field, precision=FULL)
        field = field.reshape(count, rows_n, ax, cols_n, by).transpose(1, 3, 0, 2, 4)
        return field.reshape(devices * count, ax, by)

    def backward(piece, field, precision):
        return jnp.einsum("ck,kab->abc", columns(piece), field, precision=precision)

    count = len(pieces)
    tie = lax.optimization_barrier
    fields = [forward(pieces[0])]
    arrived = [exchange(fields[0])]
    done = []
    for n in range(1, count):
        field = forward(pieces[n])
        if done:
            arrived[-1], field, done[-1] = tie((arrived[-1], field, done[-1]))
        else:
            arrived[-1], field = tie((arrived[-1], field))
        arrived.append(exchange(field))
        done.append(middle(pieces[n - 1], arrived[n - 1]))
    if done:
        arrived[-1], *done = tie((arrived[-1], *done))
    returned = []
    for n, piece in enumerate(pieces):
        if n == count - 1:
            if count > 2:
                returned[0], arrived[-1] = tie((returned[0], arrived[-1]))
            done.append(middle(piece, arrived[-1]))
        field = done[n]
        if returned:
            returned[-1], field = tie((returned[-1], field))
        returned.append(exchange(field))
    total = backward(pieces[0], returned[0], FULL)
    for piece, field in zip(pieces[1:], returned[1:]):
        total = lax.optimization_barrier(total)
        last = piece is pieces[-1]
        total = total + backward(piece, field, FAST if last else FULL)
    return total


def solution(mesh):
    placed = (P("row", "col", None), P(), P(), P(), P(), P(), P())
    return jax.shard_map(
        local, mesh=mesh, in_specs=placed, out_specs=P("row", "col", None), check_vma=False
    )
```

time: 846 us -> 824 us (0.974)
  waiting for transfers between devices: 459 us -> 382 us
  blocking collectives: 0 us -> 51 us
  matrix products: 207 us -> 230 us
  starting transfers between devices: 36.5 us -> 23.8 us
    all_to_all x8 -> x5, waiting for transfers between devices: 459 us -> 382 us  [exchange(): lax.all_to_all(field, ('row', 'col'), split_axis=0, concat_axis=0, tiled=...]
    all_to_all x0 -> x1, blocking collectives: none -> 51 us  [exchange(): lax.all_to_all(field, ('row', 'col'), split_axis=0, concat_axis=0, tiled=...]
    dot_general x24 -> x18, matrix products: 207 us -> 230 us  [the longest x3 73 us: backward(): return jnp.einsum('ck,kab->abc', columns(piece), field, precision=precision)]
    all_to_all x8 -> x5, starting transfers between devices: 36.5 us -> 23.8 us  [exchange(): lax.all_to_all(field, ('row', 'col'), split_axis=0, concat_axis=0, tiled=...]
    transpose x8 -> x6, local copies, waits for them, and re-layouts: 40.1 us -> 36.1 us  [the longest x3 18.6 us: middle(): field = jnp.einsum('xi,kiy->kxy', basis_x, field, precision=FULL)]
    reshape x13 -> x11, local copies, waits for them, and re-layouts: 74.3 us -> 72.2 us  [the longest x3 30.3 us: middle(): field = field.reshape(rows_n, cols_n, count, ax, by)]
    dot_general x4 -> x3, local copies, waits for them, and re-layouts: 17.6 us -> 17 us  [forward(): field = jnp.einsum('ck,abc->kab', columns(piece), source, precision=FAST)]
  transfers between devices with their start and end apart: 8 -> 5, of which waited for: 8 -> 5; matrix products, arithmetic and copies ran while one was open for 35% -> 39% of each run, Pallas kernels for 0% -> 0%
where the time goes in v2:
time: 824 us; the launch traced here: 818 us
  waiting for transfers between devices  382 us (46%)
  matrix products  230 us (28%)
  local copies, waits for them, and re-layouts  131 us (16%)
  blocking collectives  51 us (6%)
  starting transfers between devices  23.8 us (3%)
    all_to_all x5, waiting for transfers between devices, exchange(): lax.all_to_all(field, ('row', 'col'), split_axis=0, concat_axis=0, tiled=...  382 us
    dot_general x3, matrix products, backward(): return jnp.einsum('ck,kab->abc', columns(piece), field, precision=precision)  73 us
    all_to_all x1, blocking collectives, exchange(): lax.all_to_all(field, ('row', 'col'), split_axis=0, concat_axis=0, tiled=...  51 us
    dot_general x3, matrix products, middle(): field = jnp.einsum('xi,kxy->kiy', basis_x, field, precision=FULL)  33.5 us
    dot_general x3, matrix products, forward(): field = jnp.einsum('ck,abc->kab', columns(piece), source, precision=FAST)  33.3 us
    dot_general x3, matrix products, middle(): field = jnp.einsum('xi,kiy->kxy', basis_x, field, precision=FULL)  32.8 us
    dot_general x3, matrix products, middle(): field = jnp.einsum('kij,yj->kiy', field, basis_y, precision=FULL)  30.5 us
    reshape x3, local copies, waits for them, and re-layouts, middle(): field = field.reshape(rows_n, cols_n, count, ax, by)  30.3 us
  transfers between devices with their start and end apart: 5, of which 5 were waited for; matrix products, arithmetic and copies ran while one was open for 39% of the time, Pallas kernels for 0%

profile of v2, /device:TPU:9, one launch (start us, length us, event | category | flops | bytes accessed | tf_op | source)
XLA Modules:
  0.0 818.5 jit_solution(13178592944855999106)
XLA Ops:
  0.0 1.6 copy.59
  1.8 11.5 %fusion.41 = f32[64,64,128]{2,0,1:T(8,128)S(1)} fusion(f32[512,64,1]{0,1,2:T(8,128)S(1)} %reshape.97, f32[64,128,512]{2,1,0:T(8,128)} %param.7), kind=kOutput, calls=%fused_computation.51 | convolution fusion | flops 1610612736 | bytes 19005440 | tf_op jit(solution)/shard_map/ck,abc->kab/dot_general | solution.py:40
  13.4 2.5 copy.60
  15.9 7.0 all-to-all-start
  22.9 10.6 %fusion.40 = f32[256,64,128]{2,0,1:T(8,128)S(1)} fusion(f32[64,128,512]{2,1,0:T(8,128)} %param.7, f32[512,32,16]{0,2,1:T(8,128)} %bitcast.96), kind=kOutput, calls=%fused_computation.50 | convolution fusion | flops 6442450944 | bytes 25690112 | tf_op jit(solution)/shard_map/ck,abc->kab/dot_general | solution.py:40
  33.5 8.3 %copy.61 = f32[256,64,128]{2,1,0:T(8,128)} copy(f32[256,64,128]{2,0,1:T(8,128)S(1)} %fusion.40) | data formatting | bytes 16777216 | tf_op jit(solution)/shard_map/ck,abc->kab/dot_general | solution.py:40
  41.7 28.7 %all-to-all-done = f32[64,64,128]{2,1,0:T(8,128)S(1)} async-done(((f32[64,64,128]{2,1,0:T(8,128)}), f32[64,64,128]{2,1,0:T(8,128)S(1)}, u32[]{:S(2)}, u32[]{:S(2)}) %all-to-all-start) | async-done | bytes 2097184 | tf_op jit(solution)/shard_map/all_to_all | solution.py:37
  71.8 4.2 all-to-all-start.1
  77.2 11.2 %fusion.42 = f32[192,64,128]{2,0,1:T(8,128)S(1)} fusion(f32[512,192,1]{0,1,2:T(8,128)S(1)} %reshape.99, f32[64,128,512]{2,1,0:T(8,128)} %param.7), kind=kOutput, calls=%fused_computation.52 | convolution fusion | flops 4831838208 | bytes 23461888 | tf_op jit(solution)/shard_map/ck,abc->kab/dot_general | solution.py:40
  88.4 6.3 copy.62
  95.6 4.3 copy.107
  99.9 3.3 reshape.86
  103.2 5.0 fusion.36
  108.3 3.5 fusion.16
  111.8 3.8 fusion.20
  115.6 5.3 convolution_bitcast_fusion.2
  120.9 2.9 copy.67
  123.8 2.9 reshape.87
  126.7 3.3 copy.68
  130.0 131.9 %all-to-all-done.1 = f32[256,64,128]{2,1,0:T(8,128)} async-done(((f32[256,64,128]{2,1,0:T(8,128)}), f32[256,64,128]{2,1,0:T(8,128)}, u32[]{:S(2)}, u32[]{:S(2)}) %all-to-all-start.1) | async-done | bytes 8388640 | tf_op jit(solution)/shard_map/all_to_all | solution.py:37
  261.9 3.7 all-to-all-start.2
  265.7 14.8 %copy.105 = f32[8,4,8,64,128]{4,1,3,0,2:T(4,128)} copy(f32[8,4,8,64,128]{4,3,2,1,0:T(8,128)} %bitcast.11) | data formatting | bytes 16777216 | tf_op jit(solution)/shard_map/reshape | solution.py:45
  280.5 10.3 %reshape.90 = f32[8,512,512]{2,1,0:T(8,128)} reshape(f32[8,8,64,4,128]{4,3,2,1,0:T(4,128)} %bitcast.86) | data formatting | bytes 16777216 | tf_op jit(solution)/shard_map/reshape | solution.py:46
  290.8 15.7 %fusion.33 = f32[8,512,512]{2,1,0:T(8,128)S(1)} fusion(f32[8,512,512]{2,1,0:T(8,128)} %reshape.90, f32[512,512]{1,0:T(8,128)S(1)} %copy-done.1), kind=kOutput, calls=%fused_computation.41 | convolution fusion | flops 12884901888 | bytes 17825792 | tf_op jit(solution)/shard_map/xi,kxy->kiy/dot_general | solution.py:47
  306.4 13.6 %fusion = f32[8,512,512]{2,1,0:T(8,128)S(1)} fusion(f32[8,512,512]{2,1,0:T(8,128)S(1)} %fusion.33, f32[512,512]{1,0:T(8,128)S(1)} %copy-done), kind=kOutput, calls=%fused_computation.2 | convolution fusion | flops 12884901888 | bytes 17825792 | tf_op jit(solution)/shard_map/kiy,yj->kij/dot_general | solution.py:48
  320.0 15.2 %fusion.3 = f32[8,512,512]{1,2,0:T(8,128)S(1)} fusion(f32[8,512,512]{2,1,0:T(8,128)S(1)} %fusion, f32[8]{0:T(128)S(1)} %slice.25, f32[512,512]{1,0:T(8,128)S(1)} %broadcast_add_fusion, f32[512,512]{1,0:T(8,128)S(1)} %copy-done), kind=kOutput, calls=%fused_computation.6 | convolution fusion | flops 12889096192 | bytes 18874400 | tf_op jit(solution)/shard_map/kij,yj->kiy/dot_general | solution.py:50
  335.2 15.3 %convolution_bitcast_fusion = f32[8,512,512]{1,2,0:T(8,128)} fusion(f32[8,512,512]{1,2,0:T(8,128)S(1)} %fusion.3, f32[512,512]{1,0:T(8,128)S(1)} %copy-done.1), kind=kOutput, calls=%fused_computation.18 | convolution fusion | flops 12884901888 | bytes 17825792 | tf_op jit(solution)/shard_map/xi,kiy->kxy/dot_general | solution.py:51
  350.5 9.1 %copy.73 = f32[8,512,512]{2,1,0:T(8,128)} copy(f32[8,512,512]{1,2,0:T(8,128)} %convolution_bitcast_fusion) | data formatting | bytes 16777216 | tf_op jit(solution)/shard_map/xi,kiy->kxy/transpose | solution.py:51
  359.6 9.9 %reshape.91 = f32[8,8,64,4,128]{4,3,2,1,0:T(4,128)} reshape(f32[8,512,512]{2,1,0:T(8,128)} %copy.73) | data formatting | bytes 16777216 | tf_op jit(solution)/shard_map/reshape | solution.py:52
  369.5 7.9 copy.74
  377.4 28.3 %all-to-all-done.2 = f32[192,64,128]{2,1,0:T(8,128)} async-done(((f32[192,64,128]{2,1,0:T(8,128)}), f32[192,64,128]{2,1,0:T(8,128)}, u32[]{:S(2)}, u32[]{:S(2)}) %all-to-all-start.2) | async-done | bytes 6291488 | tf_op jit(solution)/shard_map/all_to_all | solution.py:37
  405.7 51.0 %all_to_all.30 = f32[64,64,128]{2,1,0:T(8,128)} all-to-all(f32[64,64,128]{2,1,0:T(8,128)} %bitcast.92), channel_id=1, replica_groups=mesh['row'=8,'col'=4] {'row','col'}, dimensions={0} | all-to-all | bytes 4194304 | tf_op jit(solution)/shard_map/all_to_all | solution.py:37
  456.7 5.2 all-to-all-start.4
  462.0 11.3 %copy.106 = f32[8,4,6,64,128]{4,1,3,0,2:T(4,128)} copy(f32[8,4,6,64,128]{4,3,2,1,0:T(8,128)} %bitcast.17) | data formatting | bytes 12582912 | tf_op jit(solution)/shard_map/reshape | solution.py:45
  473.2 7.8 reshape.94
  481.1 12.8 %fusion.30 = f32[6,512,512]{2,1,0:T(8,128)S(1)} fusion(f32[6,512,512]{2,1,0:T(8,128)} %reshape.94, f32[512,512]{1,0:T(8,128)S(1)} %copy-done.1), kind=kOutput, calls=%fused_computation.38 | convolution fusion | flops 9663676416 | bytes 13631488 | tf_op jit(solution)/shard_map/xi,kxy->kiy/dot_general | solution.py:47
  493.9 10.1 %fusion.6 = f32[6,512,512]{2,1,0:T(8,128)S(1)} fusion(f32[6,512,512]{2,1,0:T(8,128)S(1)} %fusion.30, f32[512,512]{1,0:T(8,128)S(1)} %copy-done), kind=kOutput, calls=%fused_computation.9 | convolution fusion | flops 9663676416 | bytes 13631488 | tf_op jit(solution)/shard_map/kiy,yj->kij/dot_general | solution.py:48
  504.0 11.5 %fusion.9 = f32[6,512,512]{1,2,0:T(8,128)S(1)} fusion(f32[6,512,512]{2,1,0:T(8,128)S(1)} %fusion.6, f32[6]{0:T(128)S(1)} %slice.26, f32[512,512]{1,0:T(8,128)S(1)} %broadcast_add_fusion, f32[512,512]{1,0:T(8,128)S(1)} %copy-done), kind=kOutput, calls=%fused_computation.13 | convolution fusion | flops 9666822144 | bytes 14680088 | tf_op jit(solution)/shard_map/kij,yj->kiy/dot_general | solution.py:50
  515.5 12.2 %convolution_bitcast_fusion.1 = f32[6,512,512]{1,2,0:T(8,128)} fusion(f32[6,512,512]{1,2,0:T(8,128)S(1)} %fusion.9, f32[512,512]{1,0:T(8,128)S(1)} %copy-done.1), kind=kOutput, calls=%fused_computation.21 | convolution fusion | flops 9663676416 | bytes 13631488 | tf_op jit(solution)/shard_map/xi,kiy->kxy/dot_general | solution.py:51
  527.8 6.5 copy.80
  534.3 7.5 reshape.95
  541.8 6.3 copy.81
  548.2 99.7 %all-to-all-done.4 = f32[256,64,128]{2,1,0:T(8,128)} async-done(((f32[256,64,128]{2,1,0:T(8,128)}), f32[256,64,128]{2,1,0:T(8,128)}, u32[]{:S(2)}, u32[]{:S(2)}) %all-to-all-start.4) | async-done | bytes 8388640 | tf_op jit(solution)/shard_map/all_to_all | solution.py:37
  647.8 3.7 all-to-all-start.5
  651.6 17.5 %fusion.18 = f32[64,128,512]{2,1,0:T(8,128)} fusion(f32[512,64,1]{0,1,2:T(8,128)} %copy-done.6, f32[64,64,128]{2,1,0:T(8,128)S(1)} %copy-done.2), kind=kOutput, calls=%fused_computation.24 | convolution fusion | flops 3221225472 | bytes 19005440 | tf_op jit(solution)/shard_map/ck,kab->abc/dot_general | solution.py:56
  669.1 28.9 %convolution_add_fusion.1 = f32[64,128,512]{2,1,0:T(8,128)} fusion(f32[64,128,512]{2,1,0:T(8,128)} %fusion.18, f32[256,64,128]{2,1,0:T(8,128)} %all-to-all-done.4, f32[512,32,16]{0,2,1:T(8,128)S(1)} %bitcast.98), kind=kOutput, calls=%fused_computation.1 | convolution fusion | flops 12889096192 | bytes 42467328 | tf_op jit(solution)/shard_map/ck,kab->abc/dot_general | solution.py:56
  698.0 93.6 %all-to-all-done.5 = f32[192,64,128]{2,1,0:T(8,128)} async-done(((f32[192,64,128]{2,1,0:T(8,128)}), f32[192,64,128]{2,1,0:T(8,128)}, u32[]{:S(2)}, u32[]{:S(2)}) %all-to-all-start.5) | async-done | bytes 6291488 | tf_op jit(solution)/shard_map/all_to_all | solution.py:37
  791.6 26.6 %convolution_add_fusion = f32[64,128,512]{2,1,0:T(8,128)} fusion(f32[64,128,512]{2,1,0:T(8,128)} %convolution_add_fusion.1, f32[512,192,1]{0,1,2:T(8,128)S(1)} %reshape.99, f32[192,64,128]{2,1,0:T(8,128)} %all-to-all-done.5), kind=kOutput, calls=%fused_computation | convolution fusion | flops 4836032512 | bytes 40239104 | tf_op jit(solution)/shard_map/ck,kab->abc/dot_general | solution.py:56
  (26 shorter events, 3.8 us)
Async XLA Ops:
  0.0 108.3 %copy-start = (f32[512,512]{1,0:T(8,128)S(1)}, f32[512,512]{1,0:T(8,128)}, u32[]{:S(2)}) copy-start(f32[512,512]{1,0:T(8,128)} %param.9) | copy-start | bytes 3145732
  1.7 11.7 %copy-start.4 = (f32[512,512]{0,1:T(8,128)}, f32[512,512]{0,1:T(8,128)S(1)}, u32[]{:S(2)}) copy-start(f32[512,512]{0,1:T(8,128)S(1)} %copy.59) | copy-start | bytes 3145732
  1.8 11.6 %copy-start.6 = (f32[512,64,1]{0,1,2:T(8,128)}, f32[512,64,1]{0,1,2:T(8,128)S(1)}, u32[]{:S(2)}) copy-start(f32[512,64,1]{0,1,2:T(8,128)S(1)} %reshape.97) | copy-start | bytes 393220
  15.9 54.5 %all-to-all-start = ((f32[64,64,128]{2,1,0:T(8,128)}), f32[64,64,128]{2,1,0:T(8,128)S(1)}, u32[]{:S(2)}, u32[]{:S(2)}) async-start(f32[64,64,128]{2,1,0:T(8,128)} %copy.60), calls=%async_computation | async-start | bytes 4194304 | tf_op jit(solution)/shard_map/all_to_all | solution.py:37
  70.4 1.3 copy-start.3
  71.8 190.1 %all-to-all-start.1 = ((f32[256,64,128]{2,1,0:T(8,128)}), f32[256,64,128]{2,1,0:T(8,128)}, u32[]{:S(2)}, u32[]{:S(2)}) async-start(f32[256,64,128]{2,1,0:T(8,128)} %copy.61), calls=%async_computation.1 | async-start | bytes 16777216 | tf_op jit(solution)/shard_map/all_to_all | solution.py:37
  88.3 7.1 copy-start.7
  88.3 7.1 copy-start.8
  94.6 8.6 %copy-start.1 = (f32[512,512]{1,0:T(8,128)S(1)}, f32[512,512]{1,0:T(8,128)}, u32[]{:S(2)}) copy-start(f32[512,512]{1,0:T(8,128)} %param.8) | copy-start | bytes 3145732
  261.9 143.8 %all-to-all-start.2 = ((f32[192,64,128]{2,1,0:T(8,128)}), f32[192,64,128]{2,1,0:T(8,128)}, u32[]{:S(2)}, u32[]{:S(2)}) async-start(f32[192,64,128]{2,1,0:T(8,128)} %copy.62), calls=%async_computation.2 | async-start | bytes 12582912 | tf_op jit(solution)/shard_map/all_to_all | solution.py:37
  456.7 191.2 %all-to-all-start.4 = ((f32[256,64,128]{2,1,0:T(8,128)}), f32[256,64,128]{2,1,0:T(8,128)}, u32[]{:S(2)}, u32[]{:S(2)}) async-start(f32[256,64,128]{2,1,0:T(8,128)} %bitcast.85), calls=%async_computation.4 | async-start | bytes 16777216 | tf_op jit(solution)/shard_map/all_to_all | solution.py:37
  647.8 3.7 copy-start.2
  647.8 143.8 %all-to-all-start.5 = ((f32[192,64,128]{2,1,0:T(8,128)}), f32[192,64,128]{2,1,0:T(8,128)}, u32[]{:S(2)}, u32[]{:S(2)}) async-start(f32[192,64,128]{2,1,0:T(8,128)} %bitcast.88), calls=%async_computation.5 | async-start | bytes 12582912 | tf_op jit(solution)/shard_map/all_to_all | solution.py:37
  651.6 17.5 %copy-start.5 = (f32[512,512]{0,1:T(8,128)S(1)}, f32[512,512]{0,1:T(8,128)}, u32[]{:S(2)}) copy-start(f32[512,512]{0,1:T(8,128)} %copy-done.4) | copy-start | bytes 3145732
